TPU v7x, 32 devices: a whole 2x2x4 slice. The times are simulated.
32 devices in a mesh: groups: 2 (over x), seq: 8 (over z, y), dec: 2 (over core).
Axes of the slice: x: 2, y: 2, z: 4, core: 2. Of those that a mesh axis runs over, the one named last changes fastest.
Arguments:
- tokens: bfloat16 [2048, 4096], P(('groups', 'seq')), parts along dimension 0, may hold values from -64 to 64
- norm_gain: float32 [4096], replicated, may hold values from 0.25 to 1.75
- w_query: bfloat16 [4096, 2048], P('seq', 'dec'), may hold values from -0.140625 to 0.140625
- w_key: bfloat16 [4096, 512], P('seq', 'dec'), may hold values from -0.140625 to 0.140625
- w_value: bfloat16 [4096, 512], P('seq', 'dec'), may hold values from -0.09375 to 0.09375
- block_order: int32 [32], P('groups'), parts along dimension 0, may hold values from 0 to 15, as said below
- block_docs: int32 [32], P('groups'), parts along dimension 0, may hold values from 0 to 3, never falling along the last dimension, each value on 1 to 8 neighbouring positions
- head_owner: int32 [8], P('groups'), parts along dimension 0, may hold values from 0 to 3, as said below
- prev_kv: bfloat16 [2048, 2, 4, 128], P(('groups', 'seq', 'dec')), parts along dimension 0, may hold values from -6 to 6
Outputs:
- attended: bfloat16 [2048, 2048], P(('groups', 'seq'), 'dec'), parts along dimension 0
- decode_cache: bfloat16 [2048, 2, 4, 128], P(('groups', 'seq'), None, 'dec'), parts along dimension 0
There are 2 independent parts, one for each index of `groups`. A program takes and returns all parts, laid end to end along the dimension named above; an argument that names none is the same for every part. Nothing has to cross between parts.
Inputs may be any that keep to these rules, and one draw needn't show every extreme that they name: `block_order`: cycle slots 2i and 2i + 1 hold the blocks b and 15 - b for some b; every block stands in exactly one slot. `head_owner`: each key-value head stands in exactly one decode slot.
All inputs are finite; a program needn't handle non-finite values.
Results may differ from a plain program's by a relative error of at most 0.0035.
The roundings to bfloat16 on the way count: a program that leaves them out, or rounds other values in their place, can miss the bound.
Values may be sent and summed in bfloat16 or wider, within the bound.
A program may use at most 64 MiB of HBM per device.

v0:
```python
import math
import jax
import jax.numpy as jnp
from jax import lax
from jax.sharding import PartitionSpec as P

HD = 128


def rotate(values, positions):
    half_width = values.shape[-1] // 2
    frequency = 500000.0 ** (-jnp.arange(half_width, dtype=jnp.float32) / half_width)
    angles = positions[:, None].astype(jnp.float32) * frequency[None, :]
    cosines = jnp.cos(angles)[:, None, :]
    sine_terms = jnp.sin(angles)[:, None, :]
    lower_half = values[..., :half_width]
    upper_half = values[..., half_width:]
    return jnp.concatenate(
        [
            lower_half * cosines - upper_half * sine_terms,
            upper_half * cosines + lower_half * sine_terms,
        ],
        -1,
    )


def per_device(
    tokens, norm_gain, w_query, w_key, w_value, block_order, block_docs, head_owner, prev_kv
):
    rows_dev = tokens.shape[0]
    block_rows = rows_dev // 2
    inputs = tokens.astype(jnp.float32)
    normed = (
        inputs * lax.rsqrt(jnp.mean(inputs * inputs, -1, keepdims=True) + 1e-05) * norm_gain
    ).astype(jnp.bfloat16)

    def add_piece(piece):
        return jnp.dot(normed, piece, preferred_element_type=jnp.float32)

    pieces = (
        lax.all_gather(w_query, "seq", axis=0, tiled=True),
        lax.all_gather(w_key, "seq", axis=0, tiled=True),
        lax.all_gather(w_value, "seq", axis=0, tiled=True),
    )
    query_full, key_full, value_full = tuple((add_piece(piece) for piece in pieces))
    total_rows = rows_dev * lax.axis_size("seq")
    row_ids = jnp.arange(total_rows, dtype=jnp.int32)
    natural = jnp.take(block_order, row_ids // block_rows)
    pos_all = natural * block_rows + row_ids % block_rows
    doc_all = jnp.take(block_docs, natural)
    offset = lax.axis_index("seq") * rows_dev
    my_pos = lax.dynamic_slice_in_dim(pos_all, offset, rows_dev)
    my_doc = lax.dynamic_slice_in_dim(doc_all, offset, rows_dev)
    local_kv = key_full.shape[1] // HD
    local_heads = query_full.shape[1] // HD
    group_size = local_heads // local_kv
    queries = rotate(query_full.reshape(rows_dev, local_heads, HD), my_pos).astype(jnp.bfloat16)
    query_groups = queries.reshape(rows_dev, local_kv, group_size, HD).transpose(1, 2, 0, 3)
    key_rows = (
        rotate(key_full.reshape(rows_dev, local_kv, HD), my_pos)
        .astype(jnp.bfloat16)
        .reshape(rows_dev, local_kv * HD)
    )
    value_rows = value_full.astype(jnp.bfloat16)
    scale = 1.0 / math.sqrt(HD)
    start_max = jnp.full((local_kv, group_size, rows_dev, 1), -jnp.inf, jnp.float32)
    start_sum = jnp.zeros((local_kv, group_size, rows_dev, 1), jnp.float32)
    start_weighted = jnp.zeros((local_kv, group_size, rows_dev, HD), jnp.float32)
    key_piece = lax.all_gather(key_rows, "seq", axis=0, tiled=True)
    value_piece = lax.all_gather(value_rows, "seq", axis=0, tiled=True)
    count = key_piece.shape[0]
    allowed = (pos_all[None, :] <= my_pos[:, None]) & (doc_all[None, :] == my_doc[:, None])

    def update(state):
        running_max, running_sum, weighted = state
        scores = (
            jnp.einsum(
                "ghtd,sgd->ghts",
                query_groups,
                key_piece.reshape(count, local_kv, HD),
                preferred_element_type=jnp.float32,
            )
            * scale
        )
        scores = jnp.where(allowed, scores, -jnp.inf)
        new_max = jnp.max(scores, -1, keepdims=True)
        shift_by = jnp.where(new_max == -jnp.inf, 0.0, new_max)
        weights = jnp.exp(scores - shift_by)
        rescale = jnp.exp(running_max - shift_by)
        running_sum = running_sum * rescale + jnp.sum(weights, -1, keepdims=True)
        weighted = weighted * rescale + jnp.einsum(
            "ghts,sgd->ghtd",
            weights.astype(jnp.bfloat16),
            value_piece.reshape(count, local_kv, HD),
            preferred_element_type=jnp.float32,
        )
        return (new_max, running_sum, weighted)

    final_max, final_sum, final_weighted = lax.cond(
        jnp.any(allowed), update, lambda state: state, (start_max, start_sum, start_weighted)
    )
    attended = (
        (final_weighted / final_sum)
        .transpose(2, 0, 1, 3)
        .reshape(rows_dev, local_heads * HD)
        .astype(jnp.bfloat16)
    )
    head_count = prev_kv.shape[2]
    selector = (head_owner[:, None] == jnp.arange(head_count, dtype=jnp.int32)[None, :]).astype(
        jnp.bfloat16
    )
    ordered = jnp.einsum(
        "tcjd,sj->tcsd", prev_kv, selector, preferred_element_type=jnp.float32
    ).astype(jnp.bfloat16)
    decode_cache = lax.all_to_all(ordered, "dec", split_axis=2, concat_axis=0, tiled=True)
    return (attended, decode_cache)


def solution(mesh):
    in_specs = (
        P(("groups", "seq"), None),
        P(),
        P("seq", "dec"),
        P("seq", "dec"),
        P("seq", "dec"),
        P("groups"),
        P("groups"),
        P("groups"),
        P(("groups", "seq", "dec"), None, None, None),
    )
    out_specs = (P(("groups", "seq"), "dec"), P(("groups", "seq"), None, "dec", None))
    return jax.shard_map(
        per_device, mesh=mesh, in_specs=in_specs, out_specs=out_specs, check_vma=False
    )
```

profile of v0, /device:TPU:0, one launch (start us, length us, event | category | flops | bytes accessed | tf_op | source)
XLA Modules:
  0.0 262.9 jit_solution(15112407311073166945)
XLA Ops:
  7.2 0.0 copy-start
  7.2 0.0 all-gather.4.cloned.1.call-start
  7.2 0.7 all-gather.4.cloned.1.call-update
  7.9 0.0 all-gather.8.cloned.1.call-start
  8.0 0.7 all-gather.8.cloned.1.call-update
  8.7 0.0 all-gather.6.cloned.1.call-start
  8.7 0.7 all-gather.6.cloned.1.call-update
  9.4 0.0 copy-start.2
  9.4 0.0 copy-start.3
  9.4 1.0 fusion.21
  10.4 0.8 copy.22
  11.2 3.4 %all-to-all-start = ((bf16[64,2,4,128]{3,1,0,2:T(2,128)(2,1)}), bf16[64,2,4,128]{3,1,0,2:T(2,128)(2,1)S(1)}, u32[]{:S(2)}, u32[]{:S(2)}) async-start(bf16[64,2,4,128]{3,1,0,2:T(2,128)(2,1)} %copy.22), calls=%async_computation | async-start | bytes 262144 | tf_op jit(solution)/shard_map/all_to_all | solution.py:115
  14.6 2.0 fusion.58
  16.6 1.9 fusion.59
  18.5 19.9 %select_select_fusion = s32[1024]{0:T(1024)S(1)} fusion(s32[]{:T(128)} %bitcast.35, s32[]{:T(128)} %bitcast.34, s32[]{:T(128)} %bitcast.33, s32[]{:T(128)} %bitcast.32, s32[]{:T(128)} %bitcast.31, s32[]{:T(128)} %bitcast.30, s32[]{:T(128)} %bitcast.29, s32[]{:T(128)} %bitcast.28, s32[]{:T(128)} %bitcast.27, s32[]{:T(128)} %bitcast.26, s32[]{:T(128)} %bitcast.25, ...), kind=kLoop, calls=%fused_computation.72 | loop fusion | flops 83968 | bytes 4224 | tf_op jit(solution)/shard_map/jit(_take)/select_n | solution.py:50
  38.4 0.1 dynamic_slice.7
  38.5 10.0 %fusion.29 = s32[1024]{0:T(1024)S(1)} fusion(s32[]{:T(128)} %bitcast.19, s32[]{:T(128)} %bitcast.18, s32[]{:T(128)} %bitcast.17, s32[]{:T(128)} %bitcast.16, s32[]{:T(128)} %bitcast.15, s32[]{:T(128)} %bitcast.14, s32[]{:T(128)} %bitcast.13, s32[]{:T(128)} %bitcast.12, s32[]{:T(128)} %bitcast.11, s32[]{:T(128)} %bitcast.10, s32[]{:T(128)} %bitcast.9, ...), kind=kLoop, calls=%fused_computation.53 | loop fusion | flops 52224 | bytes 4160 | tf_op jit(solution)/shard_map/add | solution.py:49
  48.5 0.1 fusion.56
  48.6 0.8 fusion.57
  50.0 0.0 all-to-all-done
  50.1 0.9 copy.23
  50.9 1.5 fusion.18
  52.5 0.3 multiply_cosine_fusion
  52.8 9.2 %all-gather.4.cloned.1.call-done = bf16[4096,256]{1,0:T(8,128)(2,1)} async-done(((bf16[512,256]{1,0:T(8,128)(2,1)}), bf16[4096,256]{1,0:T(8,128)(2,1)}) %all-gather.4.cloned.1.call-update) | async-done | bytes 2097168 | tf_op jit(solution)/shard_map/all_gather | solution.py:42
  62.0 2.4 fusion.54
  64.5 0.1 reshape.133
  64.5 0.3 subtract_convert_fusion.1
  64.8 0.2 pad_maximum_fusion
  65.0 32.8 %all_gather.16 = bf16[1024,256]{1,0:T(8,128)(2,1)S(1)} all-gather(bf16[128,256]{1,0:T(8,128)(2,1)S(1)} %bitcast.75), channel_id=1, replica_groups=mesh['groups'=2,'seq'=8,'dec'=2] {'seq'}, dimensions={0}, use_global_device_ids=true | all-gather | bytes 589824 | tf_op jit(solution)/shard_map/all_gather | solution.py:69
  97.8 15.3 %all-gather.8.cloned.1.call-done = bf16[4096,256]{1,0:T(8,128)(2,1)} async-done(((bf16[512,256]{1,0:T(8,128)(2,1)}), bf16[4096,256]{1,0:T(8,128)(2,1)}) %all-gather.8.cloned.1.call-update) | async-done | bytes 2097168 | tf_op jit(solution)/shard_map/all_gather | solution.py:43
  113.1 0.0 copy-done.3
  113.1 2.1 convolution_convert_fusion.1
  115.2 33.3 %all_gather.19 = bf16[1024,256]{1,0:T(8,128)(2,1)S(1)} all-gather(bf16[128,256]{1,0:T(8,128)(2,1)S(1)} %convolution_convert_fusion.1), channel_id=1, replica_groups=mesh['groups'=2,'seq'=8,'dec'=2] {'seq'}, dimensions={0}, use_global_device_ids=true | all-gather | bytes 589824 | tf_op jit(solution)/shard_map/all_gather | solution.py:70
  148.5 93.5 %all-gather.6.cloned.1.call-done = bf16[4096,1024]{1,0:T(8,128)(2,1)} async-done(((bf16[512,1024]{1,0:T(8,128)(2,1)}), bf16[4096,1024]{1,0:T(8,128)(2,1)}) %all-gather.6.cloned.1.call-update) | async-done | bytes 8388624 | tf_op jit(solution)/shard_map/all_gather | solution.py:41
  242.0 4.7 %convolution_bitcast_fusion = f32[16,8,8,128]{3,1,2,0:T(8,128)S(1)} fusion(bf16[4096,1024]{1,0:T(8,128)(2,1)} %all-gather.6.cloned.1.call-done, bf16[128,4096]{1,0:T(8,128)(2,1)S(1)} %copy-done.2, f32[4096]{0:T(1024)S(1)} %copy-done.3, f32[128]{0:T(128)S(1)} %add_rsqrt_fusion), kind=kOutput, calls=%fused_computation.25 | convolution fusion | flops 1075838976 | bytes 9978368 | tf_op jit(solution)/shard_map/dot_general | solution.py:38
  246.7 0.1 copy.32
  246.8 0.3 subtract_convert_fusion
  247.1 0.1 maximum_bitcast_fusion
  247.3 7.8 %conditional.1 = (f32[2,4,128,1]{2,1,0,3:T(4,128)S(1)}, f32[2,4,128,128]{3,2,1,0:T(8,128)S(1)}) conditional(s32[]{:T(128)} %convert_element_type.43, () %tuple.17, (pred[128,1024]{1,0:T(8,128)(4,1)S(1)}, bf16[1024,256]{1,0:T(8,128)(2,1)S(1)}, bf16[2,4,128,128]{3,2,1,0:T(8,128)(2,1)S(1)}, bf16[1024,256]{1,0:T(8,128)(2,1)S(1)}) %tuple.18), branch_computations={%region_2.4_spmd, %region_3.7_spmd} | conditional | flops 548543488 | bytes 33730604 | solution.py:99
  247.3 0.1 reshape.129
  247.4 2.8 %fusion = (f32[2,4,128]{2,1,0:T(4,128)S(1)}, f32[2,4,128,1024]{3,2,1,0:T(8,128)}) fusion(pred[128,1024]{1,0:T(8,128)(4,1)S(1)} %get-tuple-element.3, bf16[2,4,128,128]{3,2,1,0:T(8,128)(2,1)S(1)} %get-tuple-element.10, bf16[1024,2,128,1]{2,1,0,3:T(2,128)(2,1)S(1)} %bitcast.69), kind=kOutput, calls=%fused_computation.2 | convolution fusion | flops 271580160 | bytes 5115904 | tf_op jit(solution)/shard_map/cond/branch_1_fun/ghtd,sgd->ghts/dot_general | solution.py:77
  250.2 0.1 reshape.130
  250.4 0.0 copy-start.1
  250.4 3.5 %fusion.6 = f32[2,4,128,128]{3,2,1,0:T(8,128)S(1)} fusion(f32[2,4,128,1024]{3,2,1,0:T(8,128)} %get-tuple-element.26, f32[2,4,128]{2,1,0:T(4,128)S(1)} %get-tuple-element.24, pred[128,1024]{1,0:T(8,128)(4,1)S(1)} %get-tuple-element.3, bf16[1024,2,128,1]{2,1,0,3:T(2,128)(2,1)S(1)} %bitcast.72, f32[2,4,128]{2,1,0:T(4,128)S(1)} %get-tuple-element.23), kind=kOutput, calls=%fused_computation.7 | convolution fusion | flops 272760832 | bytes 5382144 | tf_op jit(solution)/shard_map/cond/branch_1_fun/ghts,sgd->ghtd/dot_general | solution.py:91
  253.9 1.1 fusion.2
  255.1 0.2 fusion.22
  255.3 0.2 copy.21
  255.5 0.9 convert_element_type.51
  (10 shorter events, 0.1 us)
Async XLA Ops:
  7.2 2.2 copy-start
  7.2 54.9 %all-gather.4.cloned.1.call-start = ((), (), s32[]{:S(2)}) async-start(), calls=%async_computation.1 | async-start | bytes 2359296 | tf_op jit(solution)/shard_map/all_gather | solution.py:42
  7.9 105.2 %all-gather.8.cloned.1.call-start = ((), (), s32[]{:S(2)}) async-start(), calls=%async_computation.3 | async-start | bytes 2359296 | tf_op jit(solution)/shard_map/all_gather | solution.py:43
  8.7 233.3 %all-gather.6.cloned.1.call-start = ((), (), s32[]{:S(2)}) async-start(), calls=%async_computation.2 | async-start | bytes 9437184 | tf_op jit(solution)/shard_map/all_gather | solution.py:41
  9.4 103.7 %copy-start.2 = (bf16[128,4096]{1,0:T(8,128)(2,1)S(1)}, bf16[128,4096]{1,0:T(8,128)(2,1)}, u32[]{:S(2)}) copy-start(bf16[128,4096]{1,0:T(8,128)(2,1)} %param.13) | copy-start | bytes 3145732
  9.4 103.7 %copy-start.3 = (f32[4096]{0:T(1024)S(1)}, f32[4096]{0:T(1024)}, u32[]{:S(2)}) copy-start(f32[4096]{0:T(1024)} %param.14) | copy-start | bytes 49156
  11.2 38.8 %all-to-all-start = ((bf16[64,2,4,128]{3,1,0,2:T(2,128)(2,1)}), bf16[64,2,4,128]{3,1,0,2:T(2,128)(2,1)S(1)}, u32[]{:S(2)}, u32[]{:S(2)}) async-start(bf16[64,2,4,128]{3,1,0,2:T(2,128)(2,1)} %copy.22), calls=%async_computation | async-start | bytes 262144 | tf_op jit(solution)/shard_map/all_to_all | solution.py:115
  250.4 3.6 %copy-start.1 = (f32[2,4,128,1024]{3,2,1,0:T(8,128)S(1)}, f32[2,4,128,1024]{3,2,1,0:T(8,128)}, u32[]{:S(2)}) copy-start(f32[2,4,128,1024]{3,2,1,0:T(8,128)} %get-tuple-element.26) | copy-start | bytes 12582916 | tf_op jit(solution)/shard_map/cond
Sparse Core Ops, SparseCore 0:
  10.1 51.8 all-gather.3
  64.2 48.8 all-gather.7
  115.2 126.7 all-gather.5
where the time goes:
time: 264 us; the launch traced here: 263 us
  waiting for transfers between devices  120 us (45%)
  blocking collectives  66.1 us (25%)
  other arithmetic  34.9 us (13%)
  matrix products  16.5 us (6%)
  between operations  14.6 us (6%)
  local copies, waits for them, and re-layouts  7.21 us (3%)
  starting transfers between devices  3.49 us (1%)
    all_gather x1, waiting for transfers between devices, per_device(): lax.all_gather(w_query, 'seq', axis=0, tiled=True)  93.5 us
    all_gather x1, blocking collectives, per_device(): value_piece = lax.all_gather(value_rows, 'seq', axis=0, tiled=True)  33.3 us
    all_gather x1, blocking collectives, per_device(): key_piece = lax.all_gather(key_rows, 'seq', axis=0, tiled=True)  32.8 us
    select_n x1, other arithmetic, per_device(): doc_all = jnp.take(block_docs, natural)  19.9 us
    all_gather x1, waiting for transfers between devices, per_device(): lax.all_gather(w_value, 'seq', axis=0, tiled=True)  15.3 us
    add x1, other arithmetic, per_device(): pos_all = natural * block_rows + row_ids % block_rows  9.98 us
    all_gather x1, waiting for transfers between devices, per_device(): lax.all_gather(w_key, 'seq', axis=0, tiled=True)  9.24 us
    dot_general x3, matrix products, add_piece(): return jnp.dot(normed, piece, preferred_element_type=jnp.float32)  9.16 us
  transfers between devices with their start and end apart: 4, of which 3 were waited for; matrix products, arithmetic and copies ran while one was open for 17% of the time, Pallas kernels for 0%

commit v1 on v0

--- a/solution.py
+++ b/solution.py
@@ -66,8 +66,11 @@
     start_max = jnp.full((local_kv, group_size, rows_dev, 1), -jnp.inf, jnp.float32)
     start_sum = jnp.zeros((local_kv, group_size, rows_dev, 1), jnp.float32)
     start_weighted = jnp.zeros((local_kv, group_size, rows_dev, HD), jnp.float32)
-    key_piece = lax.all_gather(key_rows, "seq", axis=0, tiled=True)
-    value_piece = lax.all_gather(value_rows, "seq", axis=0, tiled=True)
+    key_piece, value_piece = jnp.split(
+        lax.all_gather(jnp.concatenate([key_rows, value_rows], axis=1), "seq", axis=0, tiled=True),
+        [key_rows.shape[1]],
+        axis=1,
+    )
     count = key_piece.shape[0]
     allowed = (pos_all[None, :] <= my_pos[:, None]) & (doc_all[None, :] == my_doc[:, None])
 

time: 264 us -> 291 us (1.10)
  waiting for transfers between devices: 120 us -> 219 us
  blocking collectives: 66.1 us -> 0 us
  matrix products: 16.5 us -> 11.6 us
    all_gather x2 -> x0, blocking collectives: 66.1 us -> none  [the longest x1 33.3 us: per_device(): value_piece = lax.all_gather(value_rows, 'seq', axis=0, tiled=True)]
    all_gather x0 -> x1, waiting for transfers between devices: none -> 35.7 us  [per_device(): lax.all_gather(jnp.concatenate([key_rows, value_rows], axis=1), 'seq', ax...]
    all_gather x1, waiting for transfers between devices: 15.3 us -> 46.8 us  [per_device(): lax.all_gather(w_value, 'seq', axis=0, tiled=True)]
    all_gather x1, waiting for transfers between devices: 9.24 us -> 38.8 us  [per_device(): lax.all_gather(w_key, 'seq', axis=0, tiled=True)]
  transfers between devices with their start and end apart: 4 -> 5, of which waited for: 3 -> 4; matrix products, arithmetic and copies ran while one was open for 17% -> 16% of each run, Pallas kernels for 0% -> 0%
where the time goes in v1:
time: 291 us
  waiting for transfers between devices  219 us (75%)
  other arithmetic  35.1 us (12%)
  between operations  14.6 us (5%)
  matrix products  11.6 us (4%)
  local copies, waits for them, and re-layouts  7.28 us (3%)
  starting transfers between devices  3.53 us (1%)
    all_gather x1, waiting for transfers between devices, per_device(): lax.all_gather(w_query, 'seq', axis=0, tiled=True)  95.2 us
    all_gather x1, waiting for transfers between devices, per_device(): lax.all_gather(w_value, 'seq', axis=0, tiled=True)  46.8 us
    all_gather x1, waiting for transfers between devices, per_device(): lax.all_gather(w_key, 'seq', axis=0, tiled=True)  38.8 us
    all_gather x1, waiting for transfers between devices, per_device(): lax.all_gather(jnp.concatenate([key_rows, value_rows], axis=1), 'seq', ax...  35.7 us
    select_n x1, other arithmetic, per_device(): doc_all = jnp.take(block_docs, natural)  19.7 us
    add x1, other arithmetic, per_device(): pos_all = natural * block_rows + row_ids % block_rows  9.78 us
    dot_general x3, matrix products, add_piece(): return jnp.dot(normed, piece, preferred_element_type=jnp.float32)  9.16 us
  transfers between devices with their start and end apart: 5, of which 4 were waited for; matrix products, arithmetic and copies ran while one was open for 16% of the time, Pallas kernels for 0%

profile of v1, /device:TPU:0, one launch (start us, length us, event | category | flops | bytes accessed | tf_op | source)
XLA Modules:
  0.0 290.7 jit_solution(381813102281648015)
XLA Ops:
  7.2 0.0 copy-start
  7.2 0.0 copy-start.1
  7.2 0.0 copy-start.3
  7.2 0.0 all-gather.5.cloned.1.call-start
  7.2 0.7 all-gather.5.cloned.1.call-update
  7.9 0.0 all-gather.7.cloned.1.call-start
  8.0 0.7 all-gather.7.cloned.1.call-update
  8.7 0.0 all-gather.11.cloned.1.call-start
  8.7 0.7 all-gather.11.cloned.1.call-update
  9.4 0.0 all-gather.9.cloned.1.call-start
  9.5 1.9 fusion.56
  11.4 9.8 %fusion.26 = s32[1024]{0:T(1024)S(1)} fusion(s32[]{:T(128)} %bitcast.21, s32[]{:T(128)} %bitcast.20, s32[]{:T(128)} %bitcast.19, s32[]{:T(128)} %bitcast.18, s32[]{:T(128)} %bitcast.17, s32[]{:T(128)} %bitcast.16, s32[]{:T(128)} %bitcast.15, s32[]{:T(128)} %bitcast.14, s32[]{:T(128)} %bitcast.13, s32[]{:T(128)} %bitcast.12, s32[]{:T(128)} %bitcast.11, ...), kind=kLoop, calls=%fused_computation.51 | loop fusion | flops 52224 | bytes 4160 | tf_op jit(solution)/shard_map/add | solution.py:49
  21.2 0.1 fusion.53
  21.3 1.5 fusion.15
  22.8 0.3 multiply_cosine_fusion
  23.2 0.0 copy-start.2
  23.2 38.8 %all-gather.5.cloned.1.call-done = bf16[4096,256]{1,0:T(8,128)(2,1)} async-done(((bf16[512,256]{1,0:T(8,128)(2,1)}), bf16[4096,256]{1,0:T(8,128)(2,1)}) %all-gather.5.cloned.1.call-update) | async-done | bytes 2097168 | tf_op jit(solution)/shard_map/all_gather | solution.py:42
  62.0 2.4 fusion.51
  64.4 0.1 reshape.133
  64.5 0.3 subtract_convert_fusion.1
  64.8 0.2 pad_maximum_fusion.1
  65.0 46.8 %all-gather.7.cloned.1.call-done = bf16[4096,256]{1,0:T(8,128)(2,1)} async-done(((bf16[512,256]{1,0:T(8,128)(2,1)}), bf16[4096,256]{1,0:T(8,128)(2,1)}) %all-gather.7.cloned.1.call-update) | async-done | bytes 2097168 | tf_op jit(solution)/shard_map/all_gather | solution.py:43
  111.8 2.1 convolution_convert_fusion.1
  113.8 0.7 pad_maximum_fusion
  114.5 0.0 all-gather.9.cloned.1.call-update
  114.6 0.3 fusion.18
  114.8 0.8 copy.28
  115.6 3.4 %all-to-all-start = ((bf16[64,2,4,128]{3,1,0,2:T(2,128)(2,1)}), bf16[64,2,4,128]{3,1,0,2:T(2,128)(2,1)S(1)}, u32[]{:S(2)}, u32[]{:S(2)}) async-start(bf16[64,2,4,128]{3,1,0,2:T(2,128)(2,1)} %copy.28), calls=%async_computation | async-start | bytes 262144 | tf_op jit(solution)/shard_map/all_to_all | solution.py:118
  119.0 0.7 fusion.57
  119.7 19.7 %select_select_fusion = s32[1024]{0:T(1024)S(1)} fusion(s32[]{:T(128)} %bitcast.37, s32[]{:T(128)} %bitcast.36, s32[]{:T(128)} %bitcast.35, s32[]{:T(128)} %bitcast.34, s32[]{:T(128)} %bitcast.33, s32[]{:T(128)} %bitcast.32, s32[]{:T(128)} %bitcast.31, s32[]{:T(128)} %bitcast.30, s32[]{:T(128)} %bitcast.29, s32[]{:T(128)} %bitcast.28, s32[]{:T(128)} %bitcast.27, ...), kind=kLoop, calls=%fused_computation.70 | loop fusion | flops 83968 | bytes 4224 | tf_op jit(solution)/shard_map/jit(_take)/select_n | solution.py:50
  139.4 0.1 dynamic_slice.7
  139.5 0.8 fusion.54
  140.9 0.9 copy.29
  141.8 95.2 %all-gather.11.cloned.1.call-done = bf16[4096,1024]{1,0:T(8,128)(2,1)} async-done(((bf16[512,1024]{1,0:T(8,128)(2,1)}), bf16[4096,1024]{1,0:T(8,128)(2,1)}) %all-gather.11.cloned.1.call-update) | async-done | bytes 8388624 | tf_op jit(solution)/shard_map/all_gather | solution.py:41
  236.9 4.7 %convolution_bitcast_fusion = f32[16,8,8,128]{3,1,2,0:T(8,128)S(1)} fusion(bf16[4096,1024]{1,0:T(8,128)(2,1)} %all-gather.11.cloned.1.call-done, bf16[128,4096]{1,0:T(8,128)(2,1)S(1)} %copy-done.1, f32[4096]{0:T(1024)S(1)} %copy-done.3, f32[128]{0:T(128)S(1)} %add_rsqrt_fusion), kind=kOutput, calls=%fused_computation.22 | convolution fusion | flops 1075838976 | bytes 9978368 | tf_op jit(solution)/shard_map/dot_general | solution.py:38
  241.6 0.1 copy.38
  241.7 0.3 subtract_convert_fusion
  242.1 0.1 maximum_bitcast_fusion
  242.2 35.7 %all-gather.9.cloned.1.call-done = bf16[1024,512]{1,0:T(8,128)(2,1)} async-done(((bf16[128,512]{1,0:T(8,128)(2,1)}), bf16[1024,512]{1,0:T(8,128)(2,1)}) %all-gather.9.cloned.1.call-update) | async-done | bytes 1048592 | tf_op jit(solution)/shard_map/all_gather | solution.py:70
  278.0 4.9 %conditional.1 = (f32[2,4,128,1]{2,1,0,3:T(4,128)S(1)}, f32[2,4,128,128]{3,2,1,0:T(8,128)S(1)}) conditional(s32[]{:T(128)} %convert_element_type.43, () %tuple.17, (pred[128,1024]{1,0:T(8,128)(4,1)S(1)}, bf16[1024,512]{1,0:T(8,128)(2,1)}, bf16[2,4,128,128]{3,2,1,0:T(8,128)(2,1)S(1)}) %tuple.18), branch_computations={%region_2.4_spmd, %region_3.7_spmd} | conditional | flops 548543488 | bytes 19050512 | solution.py:102
  278.0 1.5 copy.26
  279.5 0.1 fusion.55
  279.5 0.9 fusion
  280.5 1.3 fusion.6
  281.7 1.1 fusion.2
  282.9 0.2 fusion.19
  283.1 0.2 copy.27
  283.3 0.9 convert_element_type.51
  (14 shorter events, 0.1 us)
Async XLA Ops:
  7.2 107.4 %copy-start = (bf16[64,2,4,128]{3,2,1,0:T(4,128)(2,1)S(1)}, bf16[64,2,4,128]{3,2,1,0:T(4,128)(2,1)}, u32[]{:S(2)}) copy-start(bf16[64,2,4,128]{3,2,1,0:T(4,128)(2,1)} %param.21) | copy-start | bytes 393220
  7.2 104.6 %copy-start.1 = (bf16[128,4096]{1,0:T(8,128)(2,1)S(1)}, bf16[128,4096]{1,0:T(8,128)(2,1)}, u32[]{:S(2)}) copy-start(bf16[128,4096]{1,0:T(8,128)(2,1)} %param.13) | copy-start | bytes 3145732
  7.2 104.6 %copy-start.3 = (f32[4096]{0:T(1024)S(1)}, f32[4096]{0:T(1024)}, u32[]{:S(2)}) copy-start(f32[4096]{0:T(1024)} %param.14) | copy-start | bytes 49156
  7.2 54.8 %all-gather.5.cloned.1.call-start = ((), (), s32[]{:S(2)}) async-start(), calls=%async_computation.1 | async-start | bytes 2359296 | tf_op jit(solution)/shard_map/all_gather | solution.py:42
  7.9 103.8 %all-gather.7.cloned.1.call-start = ((), (), s32[]{:S(2)}) async-start(), calls=%async_computation.2 | async-start | bytes 2359296 | tf_op jit(solution)/shard_map/all_gather | solution.py:43
  8.7 228.2 %all-gather.11.cloned.1.call-start = ((), (), s32[]{:S(2)}) async-start(), calls=%async_computation.4 | async-start | bytes 9437184 | tf_op jit(solution)/shard_map/all_gather | solution.py:41
  9.4 268.6 %all-gather.9.cloned.1.call-start = ((), (), s32[]{:S(2)}) async-start(), calls=%async_computation.3 | async-start | bytes 1179648 | tf_op jit(solution)/shard_map/all_gather | solution.py:70
  23.2 91.4 %copy-start.4 = (s32[4]{0:T(128)S(1)}, s32[4]{0:T(128)}, u32[]{:S(2)}) copy-start(s32[4]{0:T(128)} %param.20) | copy-start | bytes 52
  23.2 95.8 %copy-start.2 = (s32[16]{0:T(128)S(1)}, s32[16]{0:T(128)}, u32[]{:S(2)}) copy-start(s32[16]{0:T(128)} %param.19) | copy-start | bytes 196
  115.6 25.3 %all-to-all-start = ((bf16[64,2,4,128]{3,1,0,2:T(2,128)(2,1)}), bf16[64,2,4,128]{3,1,0,2:T(2,128)(2,1)S(1)}, u32[]{:S(2)}, u32[]{:S(2)}) async-start(bf16[64,2,4,128]{3,1,0,2:T(2,128)(2,1)} %copy.28), calls=%async_computation | async-start | bytes 262144 | tf_op jit(solution)/shard_map/all_to_all | solution.py:118
Sparse Core Ops, SparseCore 0:
  10.1 51.8 all-gather.4
  64.1 47.5 all-gather.6
  113.9 122.9 all-gather.10
  239.5 38.4 all-gather.8
